TPU v7x, 32 devices: a whole 2x2x4 slice. The times are simulated.
32 devices in a mesh: groups: 2 (over y), expert: 8 (over z, x), dp: 2 (over core).
Axes of the slice: x: 2, y: 2, z: 4, core: 2. Of those that a mesh axis runs over, the one named last changes fastest.
Arguments:
- tokens: bfloat16 [2048, 2560], P(('groups', 'expert', 'dp')), parts along dimension 0, may hold values from -6 to 6
- group_ids: int32 [2048, 2], P(('groups', 'expert', 'dp')), parts along dimension 0, may hold values from 0 to 1, as said below
- expert_ids: int32 [2048, 6], P(('groups', 'expert', 'dp')), parts along dimension 0, may hold values from 0 to 5, as said below
- gate_weights: bfloat16 [2048, 6], P(('groups', 'expert', 'dp')), parts along dimension 0, may hold values from 0.019897461 to 0.59765625
- gate_proj: bfloat16 [8, 2560, 576], P('expert', 'dp'), may hold values from -0.125 to 0.125
- up_proj: bfloat16 [8, 2560, 576], P('expert', 'dp'), may hold values from -0.125 to 0.125
- down_proj: bfloat16 [8, 2560, 576], P('expert', 'dp'), may hold values from -0.21875 to 0.21875
Outputs:
- moe_out: bfloat16 [2048, 2560], P(('groups', 'expert', 'dp')), parts along dimension 0
There are 2 independent parts, one for each index of `groups`. A program takes and returns all parts, laid end to end along the dimension named above; an argument that names none is the same for every part. Nothing has to cross between parts.
Inputs may be any that keep to these rules, and one draw needn't show every extreme that they name: `group_ids`: each row holds 2 distinct expert groups. `expert_ids`: each row holds 6 distinct experts, each of them in one of the row's groups; expert e belongs to group e // 3.
All inputs are finite; a program needn't handle non-finite values.
Results may differ from a plain program's by a relative error of at most 0.0078.
Values may be sent and summed in bfloat16 or wider, within the bound.
A program may use at most 128 MiB of HBM per device.

v0:
```python
import jax
import jax.numpy as jnp
from jax import lax
from jax.sharding import PartitionSpec as P

GROUP_EXP = 3
SPAN = 4
CAP = 8


def swapped(block, axis, distance):
    count = lax.axis_size(axis)
    route = []
    for low in range(count):
        high = low | 1 << distance
        if high != low and high < count:
            route += [(low, high), (high, low)]
    return lax.ppermute(block, axis, route)


def place_bit(bit_place):
    position = lax.axis_index("expert")
    return position // 2**bit_place % 2


def spread_rows(values):
    for bit_place in range(2):
        partner = swapped(values, "expert", bit_place)
        lower_first = jnp.concatenate([values, partner], axis=1)
        upper_first = jnp.concatenate([partner, values], axis=1)
        values = jnp.where(place_bit(bit_place) == 0, lower_first, upper_first)
    return values


def body(tokens, group_ids, expert_ids, gate_weights, gate_proj, up_proj, down_proj):
    tok_rows, width = tokens.shape
    n_expert = lax.axis_size("expert")
    n_groups = n_expert // SPAN
    slots = CAP
    cols = gate_proj.shape[2]
    hidden_slice = cols // GROUP_EXP
    whole_gate, whole_up, whole_down = (
        lax.all_gather(gate_proj, "dp", axis=1, tiled=True),
        lax.all_gather(up_proj, "dp", axis=1, tiled=True),
        lax.all_gather(down_proj, "dp", axis=1, tiled=True),
    )
    group_iota = jnp.arange(n_groups, dtype=jnp.int32)
    member = jnp.sum((group_ids[:, :, None] == group_iota).astype(jnp.int32), axis=1)
    rank = jnp.cumsum(member, axis=0) - member
    kept = member * (rank < slots).astype(jnp.int32)
    slot_iota = jnp.arange(slots, dtype=jnp.int32)
    select = (kept[:, :, None] * (rank[:, :, None] == slot_iota).astype(jnp.int32)).astype(
        jnp.bfloat16
    )
    expert_table = jnp.arange(n_groups * GROUP_EXP, dtype=jnp.int32).reshape(n_groups, GROUP_EXP)
    matches = (expert_ids[:, :, None, None] == expert_table).astype(jnp.float32)
    factor = jnp.einsum("tj,tjgk->tgk", gate_weights.astype(jnp.float32), matches)
    send_rows = jnp.einsum(
        "tgc,td->gcd", select, tokens, preferred_element_type=jnp.float32
    ).astype(jnp.bfloat16)
    send_factor = jnp.einsum("tgc,tgk->gck", select.astype(jnp.float32), factor).astype(
        jnp.bfloat16
    )
    rep_factor = jnp.broadcast_to(send_factor[:, None], (n_groups, SPAN, slots, GROUP_EXP)).reshape(
        n_expert, slots, GROUP_EXP
    )
    part_rows = send_rows.reshape(n_expert, slots // SPAN, width)
    some_rows, got_factor = (
        lax.all_to_all(part_rows, "expert", split_axis=0, concat_axis=0, tiled=True),
        lax.all_to_all(rep_factor, "expert", split_axis=0, concat_axis=0, tiled=True),
    )
    got_rows = spread_rows(some_rows)
    rows = got_rows.reshape(n_expert * slots, width)
    row_factor = got_factor.reshape(n_expert * slots, GROUP_EXP).astype(jnp.float32)
    gate_h = jnp.dot(rows, whole_gate[0], preferred_element_type=jnp.float32)
    up_h = jnp.dot(rows, whole_up[0], preferred_element_type=jnp.float32)
    active = (jax.nn.silu(gate_h) * up_h).reshape(n_expert * slots, GROUP_EXP, hidden_slice)
    hidden = (active * row_factor[:, :, None]).reshape(n_expert * slots, cols).astype(jnp.bfloat16)
    partial_value = lax.dot_general(
        hidden, whole_down[0], (((1,), (1,)), ((), ())), preferred_element_type=jnp.float32
    )
    partial_value = partial_value.reshape(n_expert, slots, width)
    returned = lax.all_to_all(partial_value, "expert", split_axis=0, concat_axis=0, tiled=True)
    group_out = jnp.sum(returned.reshape(n_groups, SPAN, slots, width), axis=1).astype(jnp.bfloat16)
    result = jnp.einsum("tgc,gcd->td", select, group_out, preferred_element_type=jnp.float32)
    return result.astype(jnp.bfloat16)


def solution(mesh):
    placed = (
        P(("groups", "expert", "dp"), None),
        P(("groups", "expert", "dp"), None),
        P(("groups", "expert", "dp"), None),
        P(("groups", "expert", "dp"), None),
        P("expert", "dp", None),
        P("expert", "dp", None),
        P("expert", "dp", None),
    )
    return jax.shard_map(
        body,
        mesh=mesh,
        in_specs=placed,
        out_specs=P(("groups", "expert", "dp"), None),
        check_vma=False,
    )
```

profile of v0, /device:TPU:0, one launch (start us, length us, event | category | flops | bytes accessed | tf_op | source)
XLA Modules:
  0.0 88.4 jit_solution(14101170514162651385)
XLA Ops:
  6.5 0.0 copy-start
  6.5 0.0 copy-start.3
  6.5 0.0 copy-start.1
  6.5 0.0 copy-start.2
  6.5 0.0 all-gather.4.cloned.1.call-start
  6.6 0.7 all-gather.4.cloned.1.call-update
  7.3 0.0 all-gather.6.cloned.1.call-start
  7.3 0.7 all-gather.6.cloned.1.call-update
  8.0 0.0 all-gather.8.cloned.1.call-start
  8.1 0.7 all-gather.8.cloned.1.call-update
  8.8 0.0 copy-done.3
  8.8 0.1 copy.36
  8.9 0.1 reduce_window_sum.11
  9.0 0.1 copy.38
  9.1 0.1 copy.40
  9.1 0.0 copy-done
  9.1 0.2 convolution_convert_fusion
  9.3 0.7 reshape.63
  10.0 7.3 %all-to-all-start = ((bf16[8,2,2560]{2,1,0:T(2,128)(2,1)}), bf16[8,2,2560]{2,1,0:T(2,128)(2,1)S(1)}, u32[]{:S(2)}, u32[]{:S(2)}) async-start(bf16[8,2,2560]{2,1,0:T(2,128)(2,1)} %reshape.63), calls=%async_computation | async-start | bytes 163840 | tf_op jit(solution)/shard_map/all_to_all | solution.py:69
  17.3 0.0 copy-done.1
  17.3 0.1 copy.41
  17.4 0.0 copy-done.2
  17.4 0.1 copy.50
  17.5 1.1 %fusion.21 = bf16[64,2,3]{2,1,0:T(2,128)(2,1)S(1)} fusion(f32[64,6]{1,0:T(8,128)S(1)} %copy.50, s32[2,3]{1,0:T(2,128)S(1)} %multiply_add_fusion, s32[64,6]{1,0:T(8,128)S(1)} %copy.41), kind=kLoop, calls=%fused_computation.16 | loop fusion | flops 6528 | bytes 3864
  18.6 5.7 %all-to-all-done = bf16[8,2,2560]{2,1,0:T(2,128)(2,1)S(1)} async-done(((bf16[8,2,2560]{2,1,0:T(2,128)(2,1)}), bf16[8,2,2560]{2,1,0:T(2,128)(2,1)S(1)}, u32[]{:S(2)}, u32[]{:S(2)}) %all-to-all-start) | async-done | bytes 81952 | tf_op jit(solution)/shard_map/all_to_all | solution.py:69
  24.3 0.3 collective-permute-start
  24.6 0.2 convolution_convert_fusion.1
  24.8 0.6 broadcast_in_dim.2
  25.4 3.3 %all-to-all-start.1 = ((bf16[8,8,3]{1,2,0:T(4,128)(2,1)}), bf16[8,8,3]{1,2,0:T(4,128)(2,1)S(1)}, u32[]{:S(2)}, u32[]{:S(2)}) async-start(bf16[8,8,3]{1,2,0:T(4,128)(2,1)} %bitcast.4), calls=%async_computation.1 | async-start | bytes 16384 | tf_op jit(solution)/shard_map/all_to_all | solution.py:70
  28.8 0.0 collective-permute-done
  28.8 0.3 maximum_select_fusion.1
  29.1 1.9 %collective-permute-start.1 = (bf16[8,4,2560]{2,1,0:T(4,128)(2,1)S(1)}, bf16[8,4,2560]{2,1,0:T(4,128)(2,1)S(1)}, u32[]{:S(2)}, u32[]{:S(2)}) collective-permute-start(bf16[8,4,2560]{2,1,0:T(4,128)(2,1)S(1)} %maximum_select_fusion.1), channel_id=1, source_target_pairs={{0,4},{4,0},{2,6},{6,2},{8,12},{12,8},{10,14},{14,10},{1,5},{5,1},... | collective-permute-start | bytes 491528 | tf_op jit(solution)/shard_map/ppermute | solution.py:18
  31.1 4.2 %all-to-all-done.1 = bf16[8,8,3]{1,2,0:T(4,128)(2,1)S(1)} async-done(((bf16[8,8,3]{1,2,0:T(4,128)(2,1)}), bf16[8,8,3]{1,2,0:T(4,128)(2,1)S(1)}, u32[]{:S(2)}, u32[]{:S(2)}) %all-to-all-start.1) | async-done | bytes 416 | tf_op jit(solution)/shard_map/all_to_all | solution.py:70
  35.3 0.1 copy.49
  35.4 0.1 mul.34
  35.6 0.2 mul.35
  35.8 0.0 collective-permute-done.1
  35.8 0.0 all-gather.4.cloned.1.call-done
  35.8 2.8 %fusion.5 = f32[64,576]{1,0:T(8,128)S(1)} fusion(bf16[1,2560,576]{1,2,0:T(8,128)(2,1)} %all-gather.4.cloned.1.call-done, bf16[8,4,2560]{2,1,0:T(4,128)(2,1)S(1)} %collective-permute-done.1, bf16[8,4,2560]{2,1,0:T(4,128)(2,1)S(1)} %maximum_select_fusion.1, pred[]{:T(512)S(6)} %eq.54), kind=kOutput, calls=%fused_computation.7 | convolution fusion | flops 190218240 | bytes 3424257 | tf_op jit(solution)/shard_map/dot_general | solution.py:75
  38.6 0.0 all-gather.6.cloned.1.call-done
  38.6 14.0 %all-gather.8.cloned.1.call-done = bf16[1,2560,576]{1,2,0:T(8,128)(2,1)} async-done(((bf16[1,1280,576]{1,2,0:T(8,128)(2,1)}), bf16[1,2560,576]{1,2,0:T(8,128)(2,1)}) %all-gather.8.cloned.1.call-update) | async-done | bytes 2949136 | tf_op jit(solution)/shard_map/all_gather | solution.py:45
  52.6 4.4 %fusion.1 = f32[8,8,2560]{2,1,0:T(8,128)S(1)} fusion(bf16[1,2560,576]{1,2,0:T(8,128)(2,1)} %all-gather.8.cloned.1.call-done, f32[64,576]{1,0:T(8,128)S(1)} %mul.35, bf16[1,2560,576]{1,2,0:T(8,128)(2,1)} %all-gather.6.cloned.1.call-done, f32[64,576]{1,0:T(8,128)S(1)} %fusion.5, bf16[8,4,2560]{2,1,0:T(4,128)(2,1)S(1)} %collective-permute-done.1, ...), kind=kOutput, calls=%fused_computation.3 | convolution fusion | flops 379219968 | bytes 7176193 | tf_op jit(solution)/shard_map/dot_general | solution.py:79
  57.1 23.7 %all_to_all.15 = f32[8,8,2560]{2,1,0:T(8,128)S(1)} all-to-all(f32[8,8,2560]{2,1,0:T(8,128)S(1)} %fusion.1), channel_id=1, replica_groups=mesh['groups'=2,'expert'=8,'dp'=2] {'expert'}, dimensions={0} | all-to-all | bytes 1310720 | tf_op jit(solution)/shard_map/all_to_all | solution.py:83
  80.8 1.0 %fusion = bf16[64,2560]{1,0:T(8,128)(2,1)} fusion(bf16[2,8,2560]{2,1,0:T(8,128)(2,1)S(1)} %bitcast_reduce_fusion, s32[64,2]{0,1:T(2,128)S(1)} %copy.40, s32[64,2]{0,1:T(2,128)S(1)} %copy.38), kind=kOutput, calls=%fused_computation.1 | convolution fusion | flops 5409792 | bytes 410624 | tf_op jit(solution)/shard_map/tgc,gcd->td/dot_general | solution.py:85
  (5 shorter events, 0.1 us)
Async XLA Ops:
  6.5 2.6 %copy-start = (bf16[64,2560]{1,0:T(8,128)(2,1)S(1)}, bf16[64,2560]{1,0:T(8,128)(2,1)}, u32[]{:S(2)}) copy-start(bf16[64,2560]{1,0:T(8,128)(2,1)} %param.7) | copy-start | bytes 983044
  6.5 2.2 %copy-start.3 = (s32[64,2]{0,1:T(2,128)S(1)}, s32[64,2]{0,1:T(2,128)}, u32[]{:S(2)}) copy-start(s32[64,2]{0,1:T(2,128)} %param.8) | copy-start | bytes 1540
  6.5 10.7 %copy-start.1 = (s32[64,6]{0,1:T(8,128)S(1)}, s32[64,6]{0,1:T(8,128)}, u32[]{:S(2)}) copy-start(s32[64,6]{0,1:T(8,128)} %param.9) | copy-start | bytes 4612
  6.5 10.8 %copy-start.2 = (bf16[64,6]{0,1:T(8,128)(2,1)S(1)}, bf16[64,6]{0,1:T(8,128)(2,1)}, u32[]{:S(2)}) copy-start(bf16[64,6]{0,1:T(8,128)(2,1)} %param.10) | copy-start | bytes 2308
  6.5 29.2 %all-gather.4.cloned.1.call-start = ((), (), s32[]{:S(2)}) async-start(), calls=%async_computation.3 | async-start | bytes 4423680 | tf_op jit(solution)/shard_map/all_gather | solution.py:43
  7.3 31.3 %all-gather.6.cloned.1.call-start = ((), (), s32[]{:S(2)}) async-start(), calls=%async_computation.4 | async-start | bytes 4423680 | tf_op jit(solution)/shard_map/all_gather | solution.py:44
  8.0 44.6 %all-gather.8.cloned.1.call-start = ((), (), s32[]{:S(2)}) async-start(), calls=%async_computation.5 | async-start | bytes 4423680 | tf_op jit(solution)/shard_map/all_gather | solution.py:45
  10.0 14.3 %all-to-all-start = ((bf16[8,2,2560]{2,1,0:T(2,128)(2,1)}), bf16[8,2,2560]{2,1,0:T(2,128)(2,1)S(1)}, u32[]{:S(2)}, u32[]{:S(2)}) async-start(bf16[8,2,2560]{2,1,0:T(2,128)(2,1)} %reshape.63), calls=%async_computation | async-start | bytes 163840 | tf_op jit(solution)/shard_map/all_to_all | solution.py:69
  24.3 4.5 %collective-permute-start = (bf16[8,2,2560]{2,1,0:T(2,128)(2,1)S(1)}, bf16[8,2,2560]{2,1,0:T(2,128)(2,1)S(1)}, u32[]{:S(2)}, u32[]{:S(2)}) collective-permute-start(bf16[8,2,2560]{2,1,0:T(2,128)(2,1)S(1)} %all-to-all-done), channel_id=1, source_target_pairs={{0,2},{2,0},{4,6},{6,4},{8,10},{10,8},{12,14},{14,12},{1,3},{3,1},... | collective-permute-start | bytes 245768 | tf_op jit(solution)/shard_map/ppermute | solution.py:18
  25.4 9.9 %all-to-all-start.1 = ((bf16[8,8,3]{1,2,0:T(4,128)(2,1)}), bf16[8,8,3]{1,2,0:T(4,128)(2,1)S(1)}, u32[]{:S(2)}, u32[]{:S(2)}) async-start(bf16[8,8,3]{1,2,0:T(4,128)(2,1)} %bitcast.4), calls=%async_computation.1 | async-start | bytes 16384 | tf_op jit(solution)/shard_map/all_to_all | solution.py:70
  29.1 6.6 %collective-permute-start.1 = (bf16[8,4,2560]{2,1,0:T(4,128)(2,1)S(1)}, bf16[8,4,2560]{2,1,0:T(4,128)(2,1)S(1)}, u32[]{:S(2)}, u32[]{:S(2)}) collective-permute-start(bf16[8,4,2560]{2,1,0:T(4,128)(2,1)S(1)} %maximum_select_fusion.1), channel_id=1, source_target_pairs={{0,4},{4,0},{2,6},{6,2},{8,12},{12,8},{10,14},{14,10},{1,5},{5,1},... | collective-permute-start | bytes 491528 | tf_op jit(solution)/shard_map/ppermute | solution.py:18
Sparse Core Ops, SparseCore 0:
  8.9 14.5 all-gather.3
  25.0 12.9 all-gather.5
  39.6 12.9 all-gather.7
where the time goes:
time: 88.7 us; the launch traced here: 88.4 us
  waiting for transfers between devices  26.1 us (29%)
  blocking collectives  23.7 us (27%)
  between operations  13.3 us (15%)
  starting transfers between devices  13 us (15%)
  matrix products  8.62 us (10%)
  local copies, waits for them, and re-layouts  2.18 us (2%)
  other arithmetic  1.54 us (2%)
    all_to_all x1, blocking collectives, body(): lax.all_to_all(partial_value, 'expert', split_axis=0, concat_axis=0, tile...  23.7 us
    all_gather x1, waiting for transfers between devices, body(): lax.all_gather(down_proj, 'dp', axis=1, tiled=True)  14 us
    all_to_all x1, starting transfers between devices, body(): lax.all_to_all(part_rows, 'expert', split_axis=0, concat_axis=0, tiled=True)  7.28 us
    all_to_all x1, waiting for transfers between devices, body(): lax.all_to_all(part_rows, 'expert', split_axis=0, concat_axis=0, tiled=True)  5.71 us
    dot_general x1, matrix products, body(): lax.dot_general(hidden, whole_down[0], (((1,), (1,)), ((), ())), preferre...  4.45 us
    all_to_all x1, waiting for transfers between devices, body(): lax.all_to_all(rep_factor, 'expert', split_axis=0, concat_axis=0, tiled=T...  4.25 us
    all_to_all x1, starting transfers between devices, body(): lax.all_to_all(rep_factor, 'expert', split_axis=0, concat_axis=0, tiled=T...  3.33 us
    dot_general x1, matrix products, body(): gate_h = jnp.dot(rows, whole_gate[0], preferred_element_type=jnp.float32)  2.81 us
  transfers between devices with their start and end apart: 7, of which 3 were waited for; matrix products, arithmetic and copies ran while one was open for 8% of the time, Pallas kernels for 0%

commit v1 on v0

v1 whole, which is shorter than its diff:
```python
import functools

import jax
import jax.numpy as jnp
from jax import lax
from jax.experimental import pallas as pl
from jax.experimental.pallas import tpu as pltpu
from jax.sharding import PartitionSpec as P

GROUP_EXP = 3
SPAN = 4
CAP = 8
LANES = 128
CHUNK = 16


def select_rows(group_ids, home, n_groups):
    tok_rows = group_ids.shape[1]
    n_rows = n_groups * CAP
    row = lax.broadcasted_iota(jnp.int32, (n_rows, tok_rows), 0)
    group = lax.rem(home + row // CAP, n_groups)
    member = jnp.zeros((n_rows, tok_rows), jnp.float32)
    for j in range(group_ids.shape[0]):
        member += (group_ids[j : j + 1, :] == group).astype(jnp.float32)
    first = lax.broadcasted_iota(jnp.int32, (tok_rows, tok_rows), 0)
    second = lax.broadcasted_iota(jnp.int32, (tok_rows, tok_rows), 1)
    earlier = (first < second).astype(jnp.bfloat16)
    rank = jnp.dot(member.astype(jnp.bfloat16), earlier, preferred_element_type=jnp.float32)
    slot = (row % CAP).astype(jnp.float32)
    return jnp.where(rank == slot, member, 0.0)


def expert_weights(expert_ids, gate_weights, home, n_groups, lanes):
    tok_rows = expert_ids.shape[1]
    row = lax.broadcasted_iota(jnp.int32, (lanes, tok_rows), 0)
    group = lax.rem(home + row // GROUP_EXP, n_groups)
    expert = jnp.where(row < n_groups * GROUP_EXP, group * GROUP_EXP + row % GROUP_EXP, -1)
    total = jnp.zeros((lanes, tok_rows), jnp.float32)
    for j in range(expert_ids.shape[0]):
        total += jnp.where(expert_ids[j : j + 1, :] == expert, gate_weights[j : j + 1, :], 0.0)
    return total


def kernel(
    n_groups, n_dp,
    gid_ref, eid_ref, gw_ref, tok_hbm, wg_hbm, wu_hbm, wd_hbm, out_ref,
    tok, wg, wu, wd, sbuf, abuf, rows, part, got_part, hid, back, shares, summed, final,
    lsem, own_sem, a_send, a_recv, b_send, b_recv, p_send, p_recv, h_send, h_recv,
    q_send, q_recv, c_send, c_recv,
):
    place = lax.axis_index("expert")
    core = lax.axis_index("dp")
    home = place // SPAN
    spot = place % SPAN
    half = tok.shape[1] // n_dp
    lanes = sbuf.shape[3] - half
    cols = wg.shape[1]
    wide = cols // GROUP_EXP

    loads = [
        pltpu.make_async_copy(src, dst, lsem.at[i])
        for i, (src, dst) in enumerate(
            [(tok_hbm, tok), (wg_hbm.at[0], wg), (wu_hbm.at[0], wu), (wd_hbm.at[0], wd)]
        )
    ]
    for load in loads:
        load.start()

    def member(dm, dd):
        return {"expert": home * SPAN + lax.rem(spot + dm, SPAN), "dp": lax.rem(core + dd, n_dp)}

    def group_peer(r):
        return {"expert": lax.rem(home + r, n_groups) * SPAN + spot, "dp": core}

    others = [(dm, dd) for dd in range(n_dp) for dm in range(SPAN) if (dm, dd) != (0, 0)]
    barrier = pltpu.get_barrier_semaphore()
    for r in range(1, n_groups):
        pl.semaphore_signal(barrier, inc=1, device_id=group_peer(r))
    for dm, dd in others:
        pl.semaphore_signal(barrier, inc=1, device_id=member(dm, dd))

    select = select_rows(gid_ref[...], home, n_groups)
    select_low = select.astype(jnp.bfloat16)
    weights = expert_weights(
        eid_ref[...], gw_ref[...].astype(jnp.float32), home, n_groups, lanes
    ).astype(jnp.bfloat16)
    factor = lax.dot_general(
        select_low, weights, (((1,), (1,)), ((), ())), preferred_element_type=jnp.float32
    )
    factor = factor.reshape(n_groups, CAP, lanes).astype(jnp.bfloat16)
    loads[0].wait()
    for h in range(n_dp):
        picked = jnp.dot(
            select_low, tok[:, h * half : (h + 1) * half], preferred_element_type=jnp.float32
        )
        sbuf[h, :, :, :half] = picked.reshape(n_groups, CAP, half).astype(jnp.bfloat16)
        sbuf[h, :, :, half:] = factor
    pl.semaphore_wait(barrier, n_groups - 1 + len(others))

    def remote(src, dst, send, recv, device):
        return pltpu.make_async_remote_copy(
            src_ref=src, dst_ref=dst, send_sem=send, recv_sem=recv,
            device_id=device, device_id_type=pl.DeviceIdType.MESH,
        )

    to_groups = [
        remote(sbuf.at[:, r], abuf.at[:, r], a_send.at[r], a_recv.at[r], group_peer(r))
        for r in range(1, n_groups)
    ]
    for copy in to_groups:
        copy.start()
    near = pl.ds(0, 1)
    far = pl.ds(1, n_groups - 1)

    def spread(src, part_rows, n):
        return [
            remote(
                src.at[lax.rem(core + dd, n_dp), part_rows], rows.at[dd, dm, part_rows],
                b_send.at[n, dd * SPAN + dm], b_recv.at[n, dd * SPAN + dm], member(dm, dd),
            )
            for dm, dd in others
        ]

    near_copies = spread(sbuf, near, 0)
    for copy in near_copies:
        copy.start()
    own_near = pltpu.make_async_copy(sbuf.at[core, near], rows.at[0, 0, near], own_sem.at[0])
    own_near.start()
    far_copies = []
    if n_groups > 1:
        for copy in to_groups:
            copy.wait_recv()
        far_copies = spread(abuf, far, 1)
        for copy in far_copies:
            copy.start()
        own_far = pltpu.make_async_copy(abuf.at[core, far], rows.at[0, 0, far], own_sem.at[1])
        own_far.start()
    loads[1].wait()
    loads[2].wait()
    loads[3].wait()
    own_near.wait()
    if n_groups > 1:
        own_far.wait()
    for copy in near_copies + far_copies:
        copy.wait_recv()

    n_units = n_dp * SPAN * n_groups
    n_rows = n_units * CAP
    half_rows = n_rows // n_dp
    units = rows.reshape(n_units, CAP, half + lanes)

    def chunked(total, step, work):
        if total <= step:
            work(0, total)
        else:

            @pl.loop(0, total // step)
            def _(i):
                work(i * step, step)

    other_core = member(0, 1)
    exchange = []
    for which, w in ((0, wg), (1, wu)):

        def project(start, size, which=which, w=w):
            block = units[pl.ds(start, size), :, :half].astype(jnp.float32)
            block = block.reshape(size * CAP, half).astype(jnp.bfloat16)
            part[which, pl.ds(pl.multiple_of(start * CAP, CAP), size * CAP), :] = jnp.dot(
                block, w[...], preferred_element_type=jnp.float32
            )

        chunked(n_units, CHUNK, project)
        copy = remote(
            part.at[which, pl.ds(half_rows, half_rows)], got_part.at[which],
            p_send.at[which], p_recv.at[which], other_core,
        )
        copy.start()
        exchange.append(copy)
    for copy in exchange:
        copy.wait_recv()

    def activate(start, size):
        count = size * CAP
        at = pl.ds(pl.multiple_of(start * CAP, CAP), count)
        gate_h = part[0, at, :] + got_part[0, at, :]
        up_h = part[1, at, :] + got_part[1, at, :]
        weight = units[pl.ds(start, size), :, half:].astype(jnp.float32).reshape(count, lanes)
        row = lax.broadcasted_iota(jnp.int32, (count, lanes), 0) + start * CAP
        lane = lax.broadcasted_iota(jnp.int32, (count, lanes), 1)
        first = row // CAP % n_groups * GROUP_EXP
        col = lax.broadcasted_iota(jnp.int32, (count, cols), 1)
        scale = jnp.zeros((count, cols), jnp.float32)
        for k in range(GROUP_EXP):
            one = jnp.sum(jnp.where(lane == first + k, weight, 0.0), axis=1, keepdims=True)
            scale = jnp.where(col // wide == k, one, scale)
        active = gate_h / (1.0 + jnp.exp(-gate_h)) * up_h
        hid[0, at, :] = (active * scale).astype(jnp.bfloat16)

    chunked(n_units // n_dp, CHUNK, activate)
    hidden_copy = remote(hid.at[0], hid.at[1], h_send, h_recv, other_core)
    hidden_copy.start()
    shares_units = back.reshape(n_units, CAP, half)

    def lower(which):
        def work(start, size):
            at = pl.ds(pl.multiple_of(start * CAP, CAP), size * CAP)
            value = lax.dot_general(
                hid[which, at, :], wd[...], (((1,), (1,)), ((), ())),
                preferred_element_type=jnp.float32,
            )
            shares_units[pl.ds(start + which * (n_units // n_dp), size)] = value.reshape(
                size, CAP, half
            ).astype(jnp.bfloat16)

        chunked(n_units // n_dp, CHUNK, work)

    returns = {}
    for dd in range(n_dp):
        if dd == 1:
            hidden_copy.wait_recv()
        lower(dd)
        for n, part_rows in ((1, far), (0, near)):
            if n == 1 and n_groups == 1:
                continue
            for dm in range(SPAN):
                if (dm, dd) == (0, 0):
                    continue
                returns[n, dm, dd] = remote(
                    back.at[dd, dm, part_rows], shares.at[dd, dm, part_rows],
                    q_send.at[n, dd * SPAN + dm], q_recv.at[n, dd * SPAN + dm],
                    member(SPAN - dm, n_dp - dd),
                )
                returns[n, dm, dd].start()

    def reduce(dd, part_rows):
        total = None
        for dm in range(SPAN):
            src = back if (dm, dd) == (0, 0) else shares
            value = src[dd, dm, part_rows].astype(jnp.float32)
            total = value if total is None else total + value
        return total.astype(jnp.bfloat16)

    homeward = []
    if n_groups > 1:
        for dm, dd in others:
            returns[1, dm, dd].wait_recv()
        for dd in range(n_dp):
            summed[dd, far] = reduce(dd, far)
        homeward = [
            remote(
                summed.at[:, r], final.at[:, r], c_send.at[r], c_recv.at[r],
                group_peer(n_groups - r),
            )
            for r in range(1, n_groups)
        ]
        for copy in homeward:
            copy.start()
    for dm, dd in others:
        returns[0, dm, dd].wait_recv()
    for dd in range(n_dp):
        final[dd, near] = reduce(dd, near)
    for copy in homeward:
        copy.wait_recv()
    for dd in range(n_dp):
        block = final[dd].astype(jnp.float32).reshape(n_groups * CAP, half).astype(jnp.bfloat16)
        value = lax.dot_general(
            select_low, block, (((0,), (0,)), ((), ())), preferred_element_type=jnp.float32
        )
        at = pl.multiple_of(lax.rem(core + dd, n_dp) * half, LANES)
        out_ref[:, pl.ds(at, half)] = value.astype(jnp.bfloat16)
    for copy in to_groups + near_copies + far_copies + exchange + [hidden_copy]:
        copy.wait_send()
    for copy in list(returns.values()) + homeward:
        copy.wait_send()


def body(tokens, group_ids, expert_ids, gate_weights, gate_proj, up_proj, down_proj):
    tok_rows, width = tokens.shape
    n_groups = lax.axis_size("expert") // SPAN
    n_dp = lax.axis_size("dp")
    half = gate_proj.shape[1]
    cols = gate_proj.shape[2]
    lanes = -(-n_groups * GROUP_EXP // LANES) * LANES
    n_rows = n_dp * SPAN * n_groups * CAP
    low, full = jnp.bfloat16, jnp.float32
    vmem = pl.BlockSpec(memory_space=pltpu.VMEM)
    hbm = pl.BlockSpec(memory_space=pl.ANY)
    dma = pltpu.SemaphoreType.DMA
    spots = n_dp * SPAN
    return pl.pallas_call(
        functools.partial(kernel, n_groups, n_dp),
        out_shape=jax.ShapeDtypeStruct((tok_rows, width), low),
        in_specs=[vmem, vmem, vmem, hbm, hbm, hbm, hbm],
        out_specs=vmem,
        scratch_shapes=[
            pltpu.VMEM((tok_rows, width), low),
            pltpu.VMEM((half, cols), low),
            pltpu.VMEM((half, cols), low),
            pltpu.VMEM((half, cols), low),
            pltpu.VMEM((n_dp, n_groups, CAP, half + lanes), low),
            pltpu.VMEM((n_dp, n_groups, CAP, half + lanes), low),
            pltpu.VMEM((n_dp, SPAN, n_groups, CAP, half + lanes), low),
            pltpu.VMEM((2, n_rows, cols), full),
            pltpu.VMEM((2, n_rows // n_dp, cols), full),
            pltpu.VMEM((n_dp, n_rows // n_dp, cols), low),
            pltpu.VMEM((n_dp, SPAN, n_groups, CAP, half), low),
            pltpu.VMEM((n_dp, SPAN, n_groups, CAP, half), low),
            pltpu.VMEM((n_dp, n_groups, CAP, half), low),
            pltpu.VMEM((n_dp, n_groups, CAP, half), low),
            dma((4,)), dma((2,)),
            dma((n_groups,)), dma((n_groups,)),
            dma((2, spots)), dma((2, spots)),
            dma((2,)), dma((2,)), dma, dma,
            dma((2, spots)), dma((2, spots)),
            dma((n_groups,)), dma((n_groups,)),
        ],
        compiler_params=pltpu.CompilerParams(
            collective_id=0, has_side_effects=True, vmem_limit_bytes=60 * 1024 * 1024
        ),
    )(group_ids.T, expert_ids.T, gate_weights.T, tokens, gate_proj, up_proj, down_proj)


def solution(mesh):
    placed = (
        P(("groups", "expert", "dp"), None),
        P(("groups", "expert", "dp"), None),
        P(("groups", "expert", "dp"), None),
        P(("groups", "expert", "dp"), None),
        P("expert", "dp", None),
        P("expert", "dp", None),
        P("expert", "dp", None),
    )
    return jax.shard_map(
        body,
        mesh=mesh,
        in_specs=placed,
        out_specs=P(("groups", "expert", "dp"), None),
        check_vma=False,
    )
```

time: 88.7 us -> 33.2 us (0.37)
  waiting for transfers between devices: 26.1 us -> 0 us
  Pallas kernels: 0 us -> 25.2 us
  blocking collectives: 23.7 us -> 0 us
  between operations: 13.3 us -> 0.01 us
  starting transfers between devices: 13 us -> 0 us
  matrix products: 8.62 us -> 0 us
  local copies, waits for them, and re-layouts: 2.18 us -> 7.8 us
  other arithmetic: 1.54 us -> 0 us
    pallas_call x0 -> x1, Pallas kernels: none -> 25.2 us  [body(): pl.pallas_call(functools.partial(kernel, n_groups, n_dp), out_shape=jax.S...]
    all_to_all x1 -> x0, blocking collectives: 23.7 us -> none  [body(): lax.all_to_all(partial_value, 'expert', split_axis=0, concat_axis=0, tile...]
    all_gather x3 -> x0, waiting for transfers between devices: 14.1 us -> none  [the longest x1 14 us: body(): lax.all_gather(down_proj, 'dp', axis=1, tiled=True)]
    all_to_all x2 -> x0, starting transfers between devices: 10.6 us -> none  [the longest x1 7.28 us: body(): lax.all_to_all(part_rows, 'expert', split_axis=0, concat_axis=0, tiled=True)]
    all_to_all x2 -> x0, waiting for transfers between devices: 9.96 us -> none  [the longest x1 5.71 us: body(): lax.all_to_all(part_rows, 'expert', split_axis=0, concat_axis=0, tiled=True)]
    dot_general x5 -> x0, matrix products: 8.62 us -> none  [the longest x1 4.45 us: body(): lax.dot_general(hidden, whole_down[0], (((1,), (1,)), ((), ())), preferre...]
    unnamed x10 -> x8, local copies, waits for them, and re-layouts: 0.21 us -> 7.8 us
    ppermute x2 -> x0, starting transfers between devices: 2.29 us -> none  [swapped(): return lax.ppermute(block, axis, route)]
  transfers between devices with their start and end apart: 7 -> 0, of which waited for: 3 -> 0; matrix products, arithmetic and copies ran while one was open for 8% -> 0% of each run, Pallas kernels for 0% -> 0%
where the time goes in v1:
time: 33.2 us; the launch traced here: 33 us
  Pallas kernels  25.2 us (76%)
  local copies, waits for them, and re-layouts  7.8 us (23%)
    pallas_call x1, Pallas kernels, body(): pl.pallas_call(functools.partial(kernel, n_groups, n_dp), out_shape=jax.S...  25.2 us
    unnamed x8, local copies, waits for them, and re-layouts  7.8 us

profile of v1, /device:TPU:0, one launch (start us, length us, event | category | flops | bytes accessed | tf_op | source)
XLA Modules:
  0.0 33.0 jit_solution(1062517977718851969)
XLA Ops:
  0.0 0.0 copy-start
  0.0 2.8 %copy.8.wg_hbm = bf16[1,1280,576]{2,1,0:T(8,128)(2,1)} copy(bf16[1,1280,576]{1,2,0:T(8,128)(2,1)} %param.11) | data formatting | bytes 2949120 | tf_op args[4]
  2.8 0.0 copy-done
  2.8 0.0 copy-start.1
  2.8 1.7 %copy.9.wu_hbm = bf16[1,1280,576]{2,1,0:T(8,128)(2,1)} copy(bf16[1,1280,576]{1,2,0:T(8,128)(2,1)S(1)} %copy-done) | data formatting | bytes 2949120 | tf_op args[5]
  4.4 0.0 copy-done.1
  4.4 1.7 %copy.10.wd_hbm = bf16[1,1280,576]{2,1,0:T(8,128)(2,1)} copy(bf16[1,1280,576]{1,2,0:T(8,128)(2,1)S(1)} %copy-done.1) | data formatting | bytes 2949120 | tf_op args[6]
  6.1 25.2 %shard_map.73 = bf16[64,2560]{1,0:T(8,128)(2,1)} custom-call(s32[2,64]{1,0:T(2,128)} %bitcast.5, s32[6,64]{1,0:T(8,128)} %bitcast.3, bf16[6,64]{1,0:T(8,128)(2,1)} %bitcast.4, bf16[64,2560]{1,0:T(8,128)(2,1)} %tok_hbm.1, bf16[1,1280,576]{2,1,0:T(8,128)(2,1)} %copy.8.wg_hbm, bf16[1,1280,576]{2,1,0:T(8,128)(2,1)} %copy.9.wu_hbm, bf16[1,1280,576]{2,1,0:T(8,128)(2,1)} %copy.10.wd_hbm), custom_call_target="tpu_custom_call" | custom-call | tf_op jit(solution)/shard_map/pallas_call | solution.py:290
  31.3 1.7 %copy.12 = bf16[64,2560]{1,0:T(8,128)(2,1)} copy(bf16[64,2560]{1,0:T(8,128)(2,1)} %shard_map.73) | data formatting | bytes 655360
Async XLA Ops:
  0.0 2.8 %copy-start = (bf16[1,1280,576]{1,2,0:T(8,128)(2,1)S(1)}, bf16[1,1280,576]{1,2,0:T(8,128)(2,1)}, u32[]{:S(2)}) copy-start(bf16[1,1280,576]{1,2,0:T(8,128)(2,1)} %param.12) | copy-start | bytes 4423684
  2.8 1.7 %copy-start.1 = (bf16[1,1280,576]{1,2,0:T(8,128)(2,1)S(1)}, bf16[1,1280,576]{1,2,0:T(8,128)(2,1)}, u32[]{:S(2)}) copy-start(bf16[1,1280,576]{1,2,0:T(8,128)(2,1)} %param.13) | copy-start | bytes 4423684

commit v2 on v1

v2 whole, which is shorter than its diff:
```python
import functools

import jax
import jax.numpy as jnp
from jax import lax
from jax.experimental import pallas as pl
from jax.experimental.pallas import tpu as pltpu
from jax.sharding import PartitionSpec as P

GROUP_EXP = 3
SPAN = 4
CAP = 8
LANES = 128


def select_rows(group_ids, home, n_groups):
    tok_rows = group_ids.shape[1]
    n_rows = n_groups * CAP
    row = lax.broadcasted_iota(jnp.int32, (n_rows, tok_rows), 0)
    group = lax.rem(home + row // CAP, n_groups)
    member = jnp.zeros((n_rows, tok_rows), jnp.float32)
    for j in range(group_ids.shape[0]):
        member += (group_ids[j : j + 1, :] == group).astype(jnp.float32)
    first = lax.broadcasted_iota(jnp.int32, (tok_rows, tok_rows), 0)
    second = lax.broadcasted_iota(jnp.int32, (tok_rows, tok_rows), 1)
    earlier = (first < second).astype(jnp.bfloat16)
    rank = jnp.dot(member.astype(jnp.bfloat16), earlier, preferred_element_type=jnp.float32)
    slot = (row % CAP).astype(jnp.float32)
    return jnp.where(rank == slot, member, 0.0)


def expert_weights(expert_ids, gate_weights, home, n_groups, lanes):
    tok_rows = expert_ids.shape[1]
    row = lax.broadcasted_iota(jnp.int32, (lanes, tok_rows), 0)
    group = lax.rem(home + row // GROUP_EXP, n_groups)
    expert = jnp.where(row < n_groups * GROUP_EXP, group * GROUP_EXP + row % GROUP_EXP, -1)
    total = jnp.zeros((lanes, tok_rows), jnp.float32)
    for j in range(expert_ids.shape[0]):
        total += jnp.where(expert_ids[j : j + 1, :] == expert, gate_weights[j : j + 1, :], 0.0)
    return total


def kernel(
    n_groups, n_dp,
    gid_ref, eid_ref, gw_ref, tok_hbm, wg_hbm, wu_hbm, wd_hbm, out_ref,
    tok, wg, wu, wd, sbuf, abuf, summed, final, near_bufs, far_bufs,
    lsem, own_sem, a_send, a_recv, b_send, b_recv, p_send, p_recv, h_send, h_recv,
    q_send, q_recv, c_send, c_recv,
):
    place = lax.axis_index("expert")
    core = lax.axis_index("dp")
    home = place // SPAN
    spot = place % SPAN
    half = tok.shape[1] // n_dp
    lanes = sbuf.shape[3] - half
    cols = wg.shape[0]
    wide = cols // GROUP_EXP

    loads = [
        pltpu.make_async_copy(src, dst, lsem.at[i])
        for i, (src, dst) in enumerate(
            [(tok_hbm, tok), (wg_hbm.at[0], wg), (wu_hbm.at[0], wu), (wd_hbm.at[0], wd)]
        )
    ]
    for load in loads:
        load.start()

    def member(dm, dd):
        return {"expert": home * SPAN + lax.rem(spot + dm, SPAN), "dp": lax.rem(core + dd, n_dp)}

    def group_peer(r):
        return {"expert": lax.rem(home + r, n_groups) * SPAN + spot, "dp": core}

    others = [(dm, dd) for dd in range(n_dp) for dm in range(SPAN) if (dm, dd) != (0, 0)]
    barrier = pltpu.get_barrier_semaphore()
    for r in range(1, n_groups):
        pl.semaphore_signal(barrier, inc=1, device_id=group_peer(r))
    for dm, dd in others:
        pl.semaphore_signal(barrier, inc=1, device_id=member(dm, dd))

    select = select_rows(gid_ref[...], home, n_groups)
    select_low = select.astype(jnp.bfloat16)
    weights = expert_weights(
        eid_ref[...], gw_ref[...].astype(jnp.float32), home, n_groups, lanes
    ).astype(jnp.bfloat16)
    factor = lax.dot_general(
        select_low, weights, (((1,), (1,)), ((), ())), preferred_element_type=jnp.float32
    )
    factor = factor.reshape(n_groups, CAP, lanes).astype(jnp.bfloat16)
    loads[0].wait()
    for h in range(n_dp):
        picked = jnp.dot(
            select_low, tok[:, h * half : (h + 1) * half], preferred_element_type=jnp.float32
        )
        sbuf[h, :, :, :half] = picked.reshape(n_groups, CAP, half).astype(jnp.bfloat16)
        sbuf[h, :, :, half:] = factor
    pl.semaphore_wait(barrier, n_groups - 1 + len(others))

    def remote(src, dst, send, recv, device):
        return pltpu.make_async_remote_copy(
            src_ref=src, dst_ref=dst, send_sem=send, recv_sem=recv,
            device_id=device, device_id_type=pl.DeviceIdType.MESH,
        )

    others.sort(key=lambda pair: pair[1])
    n_far = n_groups - 1

    def turn(dd):
        return lax.rem(core + dd, n_dp)

    to_groups = {}
    for dd in range(n_dp):
        for r in range(1, n_groups):
            to_groups[dd, r] = remote(
                sbuf.at[turn(dd), r], abuf.at[turn(dd), r - 1],
                a_send.at[dd, r - 1], a_recv.at[dd, r - 1], group_peer(r),
            )
            to_groups[dd, r].start()

    other_core = member(0, 1)
    started = list(to_groups.values())

    def begin(*args):
        copy = remote(*args)
        copy.start()
        started.append(copy)
        return copy

    def chunked(total, step, work):
        if total <= step:
            work(0, total)
        else:

            @pl.loop(0, total // step)
            def _(i):
                work(i * step, step)

    def spread(n, dd, rows):
        src = sbuf.at[turn(dd), pl.ds(0, 1)] if n == 0 else abuf.at[turn(dd)]
        copies = []
        if dd == 0:
            own = pltpu.make_async_copy(src, rows.at[0, 0], own_sem.at[n])
            own.start()
            copies.append(own)
        for dm in range(SPAN):
            if (dm, dd) != (0, 0):
                spot_at = dd * SPAN + dm
                copies.append(
                    begin(
                        src, rows.at[dd, dm], b_send.at[n, spot_at], b_recv.at[n, spot_at],
                        member(dm, dd),
                    )
                )
        return copies

    def settle(copies):
        for copy in copies:
            if copy.is_remote:
                copy.wait_recv()
            else:
                copy.wait()

    def work_on(n, first_group, count, bufs):
        rows, part, got_part, hid, back, shares = bufs
        n_units = n_dp * SPAN * count
        half_units = n_units // n_dp
        half_rows = half_units * CAP
        units = rows.reshape(n_units, CAP, half + lanes)
        back_units = back.reshape(n_units, CAP, half)
        exchange = []
        for which, w in ((0, wg), (1, wu)):

            def project(start, size, which=which, w=w):
                block = units[pl.ds(start, size), :, :half].astype(jnp.float32)
                block = block.reshape(size * CAP, half).astype(jnp.bfloat16)
                part[which, pl.ds(pl.multiple_of(start * CAP, CAP), size * CAP), :] = (
                    lax.dot_general(
                        block, w[...], (((1,), (1,)), ((), ())),
                        preferred_element_type=jnp.float32,
                    )
                )

            chunked(n_units, n_dp * SPAN, project)
            exchange.append(
                begin(
                    part.at[which, pl.ds(half_rows, half_rows)], got_part.at[which],
                    p_send.at[n, which], p_recv.at[n, which], other_core,
                )
            )
        settle(exchange)

        def activate(start, size):
            total = size * CAP
            at = pl.ds(pl.multiple_of(start * CAP, CAP), total)
            gate_h = part[0, at, :] + got_part[0, at, :]
            up_h = part[1, at, :] + got_part[1, at, :]
            weight = units[pl.ds(start, size), :, half:].astype(jnp.float32)
            weight = weight.reshape(total, lanes)
            row = lax.broadcasted_iota(jnp.int32, (total, lanes), 0) + start * CAP
            lane = lax.broadcasted_iota(jnp.int32, (total, lanes), 1)
            first = (first_group + row // CAP % count) * GROUP_EXP
            col = lax.broadcasted_iota(jnp.int32, (total, cols), 1)
            scale = jnp.zeros((total, cols), jnp.float32)
            for k in range(GROUP_EXP):
                one = jnp.sum(jnp.where(lane == first + k, weight, 0.0), axis=1, keepdims=True)
                scale = jnp.where(col // wide == k, one, scale)
            active = gate_h / (1.0 + jnp.exp(-gate_h)) * up_h
            hid[0, at, :] = (active * scale).astype(jnp.bfloat16)

        chunked(half_units, SPAN, activate)
        hidden_copy = begin(hid.at[0], hid.at[1], h_send.at[n], h_recv.at[n], other_core)

        def lower(which):
            def work(start, size):
                at = pl.ds(pl.multiple_of(start * CAP, CAP), size * CAP)
                value = jnp.dot(hid[which, at, :], wd[...], preferred_element_type=jnp.float32)
                back_units[pl.ds(start + which * half_units, size)] = value.reshape(
                    size, CAP, half
                ).astype(jnp.bfloat16)

            chunked(half_units, SPAN, work)

        returns = {}
        for dd in range(n_dp):
            if dd == 1:
                settle([hidden_copy])
            lower(dd)
            for dm in range(SPAN):
                if (dm, dd) != (0, 0):
                    spot_at = dd * SPAN + dm
                    returns[dm, dd] = begin(
                        back.at[dd, dm], shares.at[dd, dm],
                        q_send.at[n, spot_at], q_recv.at[n, spot_at],
                        member(SPAN - dm, n_dp - dd),
                    )
        return returns

    def reduce(dd, bufs, returns):
        settle([returns[dm, dd] for dm in range(SPAN) if (dm, dd) in returns])
        total = None
        for dm in range(SPAN):
            src = bufs[4] if (dm, dd) == (0, 0) else bufs[5]
            value = src[dd, dm].astype(jnp.float32)
            total = value if total is None else total + value
        return total.astype(jnp.bfloat16)

    near_copies = spread(0, 0, near_bufs[0]) + spread(0, 1, near_bufs[0])
    far_copies = []
    for dd in range(n_dp):
        settle([to_groups[dd, r] for r in range(1, n_groups)])
        far_copies += spread(1, dd, far_bufs[0])
    for load in loads[1:]:
        load.wait()
    settle(near_copies)
    near_returns = work_on(0, 0, 1, near_bufs)
    settle(far_copies)
    far_returns = work_on(1, 1, n_far, far_bufs)
    for dd in range(n_dp):
        final[dd, pl.ds(0, 1)] = reduce(dd, near_bufs, near_returns)
    homeward = []
    for dd in range(n_dp):
        summed[dd] = reduce(dd, far_bufs, far_returns)
        for r in range(1, n_groups):
            homeward.append(
                begin(
                    summed.at[dd, r - 1], final.at[dd, r], c_send.at[dd, r - 1],
                    c_recv.at[dd, r - 1], group_peer(n_groups - r),
                )
            )
    for dd in range(n_dp):
        settle(homeward[dd * n_far : (dd + 1) * n_far])
        block = final[dd].astype(jnp.float32).reshape(n_groups * CAP, half).astype(jnp.bfloat16)
        value = lax.dot_general(
            select_low, block, (((0,), (0,)), ((), ())), preferred_element_type=jnp.float32
        )
        at = pl.multiple_of(turn(dd) * half, LANES)
        out_ref[:, pl.ds(at, half)] = value.astype(jnp.bfloat16)
    for copy in started:
        copy.wait_send()


def body(tokens, group_ids, expert_ids, gate_weights, gate_proj, up_proj, down_proj):
    tok_rows, width = tokens.shape
    n_groups = lax.axis_size("expert") // SPAN
    n_dp = lax.axis_size("dp")
    half = gate_proj.shape[1]
    cols = gate_proj.shape[2]
    lanes = -(-n_groups * GROUP_EXP // LANES) * LANES
    low, full = jnp.bfloat16, jnp.float32
    vmem = pl.BlockSpec(memory_space=pltpu.VMEM)
    hbm = pl.BlockSpec(memory_space=pl.ANY)
    dma = pltpu.SemaphoreType.DMA
    spots = n_dp * SPAN

    def buffers(count):
        n_rows = n_dp * SPAN * count * CAP
        return (
            pltpu.VMEM((n_dp, SPAN, count, CAP, half + lanes), low),
            pltpu.VMEM((2, n_rows, cols), full),
            pltpu.VMEM((2, n_rows // n_dp, cols), full),
            pltpu.VMEM((n_dp, n_rows // n_dp, cols), low),
            pltpu.VMEM((n_dp, SPAN, count, CAP, half), low),
            pltpu.VMEM((n_dp, SPAN, count, CAP, half), low),
        )

    return pl.pallas_call(
        functools.partial(kernel, n_groups, n_dp),
        out_shape=jax.ShapeDtypeStruct((tok_rows, width), low),
        in_specs=[vmem, vmem, vmem, hbm, hbm, hbm, hbm],
        out_specs=vmem,
        scratch_shapes=[
            pltpu.VMEM((tok_rows, width), low),
            pltpu.VMEM((cols, half), low),
            pltpu.VMEM((cols, half), low),
            pltpu.VMEM((cols, half), low),
            pltpu.VMEM((n_dp, n_groups, CAP, half + lanes), low),
            pltpu.VMEM((n_dp, n_groups - 1, CAP, half + lanes), low),
            pltpu.VMEM((n_dp, n_groups - 1, CAP, half), low),
            pltpu.VMEM((n_dp, n_groups, CAP, half), low),
            buffers(1),
            buffers(n_groups - 1),
            dma((4,)), dma((2,)),
            dma((n_dp, n_groups - 1)), dma((n_dp, n_groups - 1)),
            dma((2, spots)), dma((2, spots)),
            dma((2, 2)), dma((2, 2)), dma((2,)), dma((2,)),
            dma((2, spots)), dma((2, spots)),
            dma((n_dp, n_groups - 1)), dma((n_dp, n_groups - 1)),
        ],
        compiler_params=pltpu.CompilerParams(
            collective_id=0, has_side_effects=True, vmem_limit_bytes=60 * 1024 * 1024
        ),
    )(group_ids.T, expert_ids.T, gate_weights.T, tokens,
      *(jnp.swapaxes(w, 1, 2) for w in (gate_proj, up_proj, down_proj)))


def solution(mesh):
    placed = (
        P(("groups", "expert", "dp"), None),
        P(("groups", "expert", "dp"), None),
        P(("groups", "expert", "dp"), None),
        P(("groups", "expert", "dp"), None),
        P("expert", "dp", None),
        P("expert", "dp", None),
        P("expert", "dp", None),
    )
    return jax.shard_map(
        body,
        mesh=mesh,
        in_specs=placed,
        out_specs=P(("groups", "expert", "dp"), None),
        check_vma=False,
    )
```

time: 33.2 us -> 28.5 us (0.86)
  local copies, waits for them, and re-layouts: 7.8 us -> 1.72 us
  Pallas kernels: 25.2 us -> 26.6 us
    unnamed x8 -> x1, local copies, waits for them, and re-layouts: 7.8 us -> 1.72 us
    pallas_call x1, Pallas kernels: 25.2 us -> 26.6 us  [body(): pl.pallas_call(functools.partial(kernel, n_groups, n_dp), out_shape=jax.S...]
where the time goes in v2:
time: 28.5 us; the launch traced here: 28.4 us
  Pallas kernels  26.6 us (93%)
  local copies, waits for them, and re-layouts  1.72 us (6%)
    pallas_call x1, Pallas kernels, body(): pl.pallas_call(functools.partial(kernel, n_groups, n_dp), out_shape=jax.S...  26.6 us
    unnamed x1, local copies, waits for them, and re-layouts  1.72 us

profile of v2, /device:TPU:0, one launch (start us, length us, event | category | flops | bytes accessed | tf_op | source)
XLA Modules:
  0.0 28.4 jit_solution(7754732409133233506)
XLA Ops:
  0.0 26.6 %shard_map.73 = bf16[64,2560]{1,0:T(8,128)(2,1)} custom-call(s32[2,64]{1,0:T(2,128)} %bitcast.11, s32[6,64]{1,0:T(8,128)} %bitcast.9, bf16[6,64]{1,0:T(8,128)(2,1)} %bitcast.10, bf16[64,2560]{1,0:T(8,128)(2,1)} %tok_hbm.1, bf16[1,576,1280]{2,1,0:T(8,128)(2,1)} %bitcast.6, bf16[1,576,1280]{2,1,0:T(8,128)(2,1)} %bitcast.7, bf16[1,576,1280]{2,1,0:T(8,128)(2,1)} %bitcast.8), custom_call_target="tpu_custom_call" | custom-call | tf_op jit(solution)/shard_map/pallas_call | solution.py:306
  26.6 1.7 %copy.9 = bf16[64,2560]{1,0:T(8,128)(2,1)} copy(bf16[64,2560]{1,0:T(8,128)(2,1)} %shard_map.73) | data formatting | bytes 655360

commit v3 on v2

--- a/solution.py
+++ b/solution.py
@@ -42,7 +42,7 @@
 
 def kernel(
     n_groups, n_dp,
-    gid_ref, eid_ref, gw_ref, tok_hbm, wg_hbm, wu_hbm, wd_hbm, out_ref,
+    gid_ref, eid_ref, gw_ref, tok_hbm, wg_hbm, wu_hbm, wd_hbm, out_ref, select_ref,
     tok, wg, wu, wd, sbuf, abuf, summed, final, near_bufs, far_bufs,
     lsem, own_sem, a_send, a_recv, b_send, b_recv, p_send, p_recv, h_send, h_recv,
     q_send, q_recv, c_send, c_recv,
@@ -80,6 +80,7 @@
 
     select = select_rows(gid_ref[...], home, n_groups)
     select_low = select.astype(jnp.bfloat16)
+    select_ref[...] = select_low
     weights = expert_weights(
         eid_ref[...], gw_ref[...].astype(jnp.float32), home, n_groups, lanes
     ).astype(jnp.bfloat16)
@@ -269,14 +270,21 @@
             )
     for dd in range(n_dp):
         settle(homeward[dd * n_far : (dd + 1) * n_far])
-        block = final[dd].astype(jnp.float32).reshape(n_groups * CAP, half).astype(jnp.bfloat16)
-        value = lax.dot_general(
-            select_low, block, (((0,), (0,)), ((), ())), preferred_element_type=jnp.float32
-        )
-        at = pl.multiple_of(turn(dd) * half, LANES)
-        out_ref[:, pl.ds(at, half)] = value.astype(jnp.bfloat16)
+        out_ref[dd] = final[dd]
     for copy in started:
         copy.wait_send()
+
+
+def combine(n_dp, parts_ref, select_ref, out_ref):
+    core = lax.axis_index("dp")
+    half = parts_ref.shape[3]
+    for dd in range(n_dp):
+        block = parts_ref[dd].astype(jnp.float32).reshape(-1, half).astype(jnp.bfloat16)
+        value = lax.dot_general(
+            select_ref[...], block, (((0,), (0,)), ((), ())), preferred_element_type=jnp.float32
+        )
+        at = pl.multiple_of(lax.rem(core + dd, n_dp) * half, LANES)
+        out_ref[:, pl.ds(at, half)] = value.astype(jnp.bfloat16)
 
 
 def body(tokens, group_ids, expert_ids, gate_weights, gate_proj, up_proj, down_proj):
@@ -303,11 +311,14 @@
             pltpu.VMEM((n_dp, SPAN, count, CAP, half), low),
         )
 
-    return pl.pallas_call(
+    parts, select = pl.pallas_call(
         functools.partial(kernel, n_groups, n_dp),
-        out_shape=jax.ShapeDtypeStruct((tok_rows, width), low),
+        out_shape=(
+            jax.ShapeDtypeStruct((n_dp, n_groups, CAP, half), low),
+            jax.ShapeDtypeStruct((n_groups * CAP, tok_rows), low),
+        ),
         in_specs=[vmem, vmem, vmem, hbm, hbm, hbm, hbm],
-        out_specs=vmem,
+        out_specs=(vmem, vmem),
         scratch_shapes=[
             pltpu.VMEM((tok_rows, width), low),
             pltpu.VMEM((cols, half), low),
@@ -331,6 +342,12 @@
         ),
     )(group_ids.T, expert_ids.T, gate_weights.T, tokens,
       *(jnp.swapaxes(w, 1, 2) for w in (gate_proj, up_proj, down_proj)))
+    return pl.pallas_call(
+        functools.partial(combine, n_dp),
+        out_shape=jax.ShapeDtypeStruct((tok_rows, width), low),
+        in_specs=[vmem, vmem],
+        out_specs=vmem,
+    )(parts, select)
 
 
 def solution(mesh):

time: 28.5 us -> 28.5 us (level)
  local copies, waits for them, and re-layouts: 1.72 us -> 0 us
  Pallas kernels: 26.6 us -> 28.3 us
    unnamed x1 -> x0, local copies, waits for them, and re-layouts: 1.72 us -> none
    pallas_call x1 -> x2, Pallas kernels: 26.6 us -> 28.3 us  [the longest x1 26.4 us: body(): pl.pallas_call(functools.partial(kernel, n_groups, n_dp), out_shape=(jax....]
where the time goes in v3:
time: 28.5 us; the launch traced here: 28.3 us
  Pallas kernels  28.3 us (99%)
    pallas_call x1, Pallas kernels, body(): pl.pallas_call(functools.partial(kernel, n_groups, n_dp), out_shape=(jax....  26.4 us
    pallas_call x1, Pallas kernels, body(): pl.pallas_call(functools.partial(combine, n_dp), out_shape=jax.ShapeDtype...  1.89 us

profile of v3, /device:TPU:0, one launch (start us, length us, event | category | flops | bytes accessed | tf_op | source)
XLA Modules:
  0.0 28.3 jit_solution(855753241707647552)
XLA Ops:
  0.0 26.4 %shard_map.73 = (bf16[2,2,8,1280]{3,2,1,0:T(8,128)(2,1)}, bf16[16,64]{1,0:T(8,128)(2,1)}) custom-call(s32[2,64]{1,0:T(2,128)} %bitcast.11, s32[6,64]{1,0:T(8,128)} %bitcast.9, bf16[6,64]{1,0:T(8,128)(2,1)} %bitcast.10, bf16[64,2560]{1,0:T(8,128)(2,1)} %tok_hbm.1, bf16[1,576,1280]{2,1,0:T(8,128)(2,1)} %bitcast.6, bf16[1,576,1280]{2,1,0:T(8,128)(2,1)} %bitcast.7, ...), custom_call_target="tpu_custom_call" | custom-call | tf_op jit(solution)/shard_map/pallas_call | solution.py:314
  26.4 1.9 %shard_map.74 = bf16[64,2560]{1,0:T(8,128)(2,1)} custom-call(bf16[2,2,8,1280]{3,2,1,0:T(8,128)(2,1)} %get-tuple-element.7.parts_ref, bf16[16,64]{1,0:T(8,128)(2,1)} %get-tuple-element.8.select_ref), custom_call_target="tpu_custom_call" | custom-call | tf_op jit(solution)/shard_map/pallas_call | solution.py:345

commit v4 on v2

--- a/solution.py
+++ b/solution.py
@@ -42,7 +42,7 @@
 
 def kernel(
     n_groups, n_dp,
-    gid_ref, eid_ref, gw_ref, tok_hbm, wg_hbm, wu_hbm, wd_hbm, out_ref,
+    gid_ref, eid_ref, gw_ref, tok_hbm, wg_hbm, wu_hbm, wd_hbm, out_ref, select_ref,
     tok, wg, wu, wd, sbuf, abuf, summed, final, near_bufs, far_bufs,
     lsem, own_sem, a_send, a_recv, b_send, b_recv, p_send, p_recv, h_send, h_recv,
     q_send, q_recv, c_send, c_recv,
@@ -80,6 +80,7 @@
 
     select = select_rows(gid_ref[...], home, n_groups)
     select_low = select.astype(jnp.bfloat16)
+    select_ref[...] = select_low
     weights = expert_weights(
         eid_ref[...], gw_ref[...].astype(jnp.float32), home, n_groups, lanes
     ).astype(jnp.bfloat16)
@@ -269,12 +270,9 @@
             )
     for dd in range(n_dp):
         settle(homeward[dd * n_far : (dd + 1) * n_far])
-        block = final[dd].astype(jnp.float32).reshape(n_groups * CAP, half).astype(jnp.bfloat16)
-        value = lax.dot_general(
-            select_low, block, (((0,), (0,)), ((), ())), preferred_element_type=jnp.float32
-        )
         at = pl.multiple_of(turn(dd) * half, LANES)
-        out_ref[:, pl.ds(at, half)] = value.astype(jnp.bfloat16)
+        block = final[dd].astype(jnp.float32).reshape(n_groups * CAP, half)
+        out_ref[:, pl.ds(at, half)] = block.astype(jnp.bfloat16)
     for copy in started:
         copy.wait_send()
 
@@ -303,11 +301,14 @@
             pltpu.VMEM((n_dp, SPAN, count, CAP, half), low),
         )
 
-    return pl.pallas_call(
+    parts, select = pl.pallas_call(
         functools.partial(kernel, n_groups, n_dp),
-        out_shape=jax.ShapeDtypeStruct((tok_rows, width), low),
+        out_shape=(
+            jax.ShapeDtypeStruct((n_groups * CAP, width), low),
+            jax.ShapeDtypeStruct((n_groups * CAP, tok_rows), low),
+        ),
         in_specs=[vmem, vmem, vmem, hbm, hbm, hbm, hbm],
-        out_specs=vmem,
+        out_specs=(vmem, vmem),
         scratch_shapes=[
             pltpu.VMEM((tok_rows, width), low),
             pltpu.VMEM((cols, half), low),
@@ -331,6 +332,10 @@
         ),
     )(group_ids.T, expert_ids.T, gate_weights.T, tokens,
       *(jnp.swapaxes(w, 1, 2) for w in (gate_proj, up_proj, down_proj)))
+    result = lax.dot_general(
+        select, parts, (((0,), (0,)), ((), ())), preferred_element_type=jnp.float32
+    )
+    return result.astype(low)
 
 
 def solution(mesh):

time: 28.5 us -> 28.5 us (level)
  matrix products: 0 us -> 1.89 us
  local copies, waits for them, and re-layouts: 1.72 us -> 0 us
    dot_general x0 -> x1, matrix products: none -> 1.89 us  [body(): lax.dot_general(select, parts, (((0,), (0,)), ((), ())), preferred_elemen...]
    unnamed x1 -> x0, local copies, waits for them, and re-layouts: 1.72 us -> none
where the time goes in v4:
time: 28.5 us; the launch traced here: 28.3 us
  Pallas kernels  26.4 us (93%)
  matrix products  1.89 us (7%)
    pallas_call x1, Pallas kernels, body(): pl.pallas_call(functools.partial(kernel, n_groups, n_dp), out_shape=(jax....  26.4 us
    dot_general x1, matrix products, body(): lax.dot_general(select, parts, (((0,), (0,)), ((), ())), preferred_elemen...  1.89 us

profile of v4, /device:TPU:0, one launch (start us, length us, event | category | flops | bytes accessed | tf_op | source)
XLA Modules:
  0.0 28.3 jit_solution(11040209630328509463)
XLA Ops:
  0.0 26.4 %shard_map.73 = (bf16[16,2560]{1,0:T(8,128)(2,1)}, bf16[16,64]{1,0:T(8,128)(2,1)}) custom-call(s32[2,64]{1,0:T(2,128)} %bitcast.13, s32[6,64]{1,0:T(8,128)} %bitcast.11, bf16[6,64]{1,0:T(8,128)(2,1)} %bitcast.12, bf16[64,2560]{1,0:T(8,128)(2,1)} %tok_hbm.1, bf16[1,576,1280]{2,1,0:T(8,128)(2,1)} %bitcast.8, bf16[1,576,1280]{2,1,0:T(8,128)(2,1)} %bitcast.9, ...), custom_call_target="tpu_custom_call" | custom-call | tf_op jit(solution)/shard_map/pallas_call | solution.py:304
  26.4 1.9 %convolution_convert_fusion = bf16[64,2560]{1,0:T(8,128)(2,1)} fusion(bf16[16,64]{1,0:T(8,128)(2,1)} %get-tuple-element.7, bf16[16,2560]{1,0:T(8,128)(2,1)} %get-tuple-element.8), kind=kOutput, calls=%fused_computation | convolution fusion | flops 5406720 | bytes 411648 | tf_op jit(solution)/shard_map/dot_general | solution.py:335

commit v5 on v4

v5 whole, which is shorter than its diff:
```python
import functools

import jax
import jax.numpy as jnp
from jax import lax
from jax.experimental import pallas as pl
from jax.experimental.pallas import tpu as pltpu
from jax.sharding import PartitionSpec as P

GROUP_EXP = 3
SPAN = 4
CAP = 8
LANES = 128


def select_rows(group_ids, home, n_groups):
    tok_rows = group_ids.shape[1]
    n_rows = n_groups * CAP
    row = lax.broadcasted_iota(jnp.int32, (n_rows, tok_rows), 0)
    group = lax.rem(home + row // CAP, n_groups)
    member = jnp.zeros((n_rows, tok_rows), jnp.float32)
    for j in range(group_ids.shape[0]):
        member += (group_ids[j : j + 1, :] == group).astype(jnp.float32)
    first = lax.broadcasted_iota(jnp.int32, (tok_rows, tok_rows), 0)
    second = lax.broadcasted_iota(jnp.int32, (tok_rows, tok_rows), 1)
    earlier = (first < second).astype(jnp.bfloat16)
    rank = jnp.dot(member.astype(jnp.bfloat16), earlier, preferred_element_type=jnp.float32)
    slot = (row % CAP).astype(jnp.float32)
    return jnp.where(rank == slot, member, 0.0)


def expert_weights(expert_ids, gate_weights, home, n_groups, lanes):
    tok_rows = expert_ids.shape[1]
    row = lax.broadcasted_iota(jnp.int32, (lanes, tok_rows), 0)
    group = lax.rem(home + row // GROUP_EXP, n_groups)
    expert = jnp.where(row < n_groups * GROUP_EXP, group * GROUP_EXP + row % GROUP_EXP, -1)
    total = jnp.zeros((lanes, tok_rows), jnp.float32)
    for j in range(expert_ids.shape[0]):
        total += jnp.where(expert_ids[j : j + 1, :] == expert, gate_weights[j : j + 1, :], 0.0)
    return total


def kernel(
    n_groups, n_dp,
    gid_ref, eid_ref, gw_ref, tok_hbm, wg_hbm, wu_hbm, wd_hbm, out_ref, select_ref,
    tok, wg, wu, wd, sbuf, abuf, summed, final, near_bufs, far_bufs,
    lsem, own_sem, a_send, a_recv, b_send, b_recv, w_send, w_recv,
    q_send, q_recv, c_send, c_recv,
):
    place = lax.axis_index("expert")
    core = lax.axis_index("dp")
    home = place // SPAN
    spot = place % SPAN
    half = tok.shape[1] // n_dp
    width = tok.shape[1]
    lanes = sbuf.shape[2] - width
    cols = wg.shape[1]
    wide = cols // GROUP_EXP

    loads = [
        pltpu.make_async_copy(src, dst, lsem.at[i])
        for i, (src, dst) in enumerate(
            [
                (tok_hbm, tok), (wg_hbm.at[0], wg.at[core]), (wu_hbm.at[0], wu.at[core]),
                (wd_hbm.at[0], wd.at[core]),
            ]
        )
    ]
    for load in loads:
        load.start()

    def member(dm, dd):
        return {"expert": home * SPAN + lax.rem(spot + dm, SPAN), "dp": lax.rem(core + dd, n_dp)}

    def group_peer(r):
        return {"expert": lax.rem(home + r, n_groups) * SPAN + spot, "dp": core}

    others = [(dm, 0) for dm in range(1, SPAN)] + [(0, dd) for dd in range(1, n_dp)]
    barrier = pltpu.get_barrier_semaphore()
    for r in range(1, n_groups):
        pl.semaphore_signal(barrier, inc=1, device_id=group_peer(r))
    for dm, dd in others:
        pl.semaphore_signal(barrier, inc=1, device_id=member(dm, dd))

    select = select_rows(gid_ref[...], home, n_groups)
    select_low = select.astype(jnp.bfloat16)
    select_ref[...] = select_low
    weights = expert_weights(
        eid_ref[...], gw_ref[...].astype(jnp.float32), home, n_groups, lanes
    ).astype(jnp.bfloat16)
    factor = lax.dot_general(
        select_low, weights, (((1,), (1,)), ((), ())), preferred_element_type=jnp.float32
    )
    factor = factor.reshape(n_groups, CAP, lanes).astype(jnp.bfloat16)
    loads[0].wait()
    picked = jnp.dot(select_low, tok[...], preferred_element_type=jnp.float32)
    sbuf[:, :, :width] = picked.reshape(n_groups, CAP, width).astype(jnp.bfloat16)
    sbuf[:, :, width:] = factor
    pl.semaphore_wait(barrier, n_groups - 1 + len(others))

    def remote(src, dst, send, recv, device):
        return pltpu.make_async_remote_copy(
            src_ref=src, dst_ref=dst, send_sem=send, recv_sem=recv,
            device_id=device, device_id_type=pl.DeviceIdType.MESH,
        )

    n_far = n_groups - 1
    started = []

    def begin(*args):
        copy = remote(*args)
        copy.start()
        started.append(copy)
        return copy

    pieces = [pl.ds(0, half), pl.ds(half, width - half + lanes)]
    to_groups = {}
    for p, piece in enumerate(pieces):
        for r in range(1, n_groups):
            to_groups[p, r] = begin(
                sbuf.at[r, :, piece], abuf.at[r - 1, :, piece],
                a_send.at[p, r - 1], a_recv.at[p, r - 1], group_peer(r),
            )

    def chunked(total, step, work):
        if total <= step:
            work(0, total)
        else:

            @pl.loop(0, total // step)
            def _(i):
                work(i * step, step)

    def spread(n, p, rows):
        src = sbuf.at[pl.ds(0, 1), :, pieces[p]] if n == 0 else abuf.at[:, :, pieces[p]]
        own = pltpu.make_async_copy(src, rows.at[0, :, :, pieces[p]], own_sem.at[n, p])
        own.start()
        copies = [own]
        for dm in range(1, SPAN):
            copies.append(
                begin(
                    src, rows.at[dm, :, :, pieces[p]], b_send.at[n, p * SPAN + dm],
                    b_recv.at[n, p * SPAN + dm], member(dm, 0),
                )
            )
        return copies

    def settle(copies):
        for copy in copies:
            if copy.is_remote:
                copy.wait_recv()
            else:
                copy.wait()

    def work_on(n, first_group, count, bufs):
        rows, part, hid, back, shares = bufs
        n_units = SPAN * count
        units = rows.reshape(n_units, CAP, width + lanes)
        back_units = back.reshape(n_dp, n_units, CAP, half)

        def project(start, size):
            block = units[pl.ds(start, size), :, :width].astype(jnp.float32)
            block = block.reshape(size * CAP, width).astype(jnp.bfloat16)
            for which, w in ((0, wg), (1, wu)):
                total = None
                for h in range(n_dp):
                    value = lax.dot_general(
                        block[:, h * half : (h + 1) * half], w[h], (((1,), (1,)), ((), ())),
                        preferred_element_type=jnp.float32,
                    )
                    total = value if total is None else total + value
                at = pl.ds(pl.multiple_of(start * CAP, CAP), size * CAP)
                part[which, at, :] = total

        chunked(n_units, SPAN, project)

        def activate(start, size):
            total = size * CAP
            at = pl.ds(pl.multiple_of(start * CAP, CAP), total)
            gate_h = part[0, at, :]
            up_h = part[1, at, :]
            weight = units[pl.ds(start, size), :, width:].astype(jnp.float32)
            weight = weight.reshape(total, lanes)
            row = lax.broadcasted_iota(jnp.int32, (total, lanes), 0) + start * CAP
            lane = lax.broadcasted_iota(jnp.int32, (total, lanes), 1)
            first = (first_group + row // CAP % count) * GROUP_EXP
            col = lax.broadcasted_iota(jnp.int32, (total, cols), 1)
            scale = jnp.zeros((total, cols), jnp.float32)
            for k in range(GROUP_EXP):
                one = jnp.sum(jnp.where(lane == first + k, weight, 0.0), axis=1, keepdims=True)
                scale = jnp.where(col // wide == k, one, scale)
            active = gate_h / (1.0 + jnp.exp(-gate_h)) * up_h
            hid[at, :] = (active * scale).astype(jnp.bfloat16)

        chunked(n_units, SPAN, activate)
        returns = {}
        for h in range(n_dp):

            def lower(start, size, h=h):
                at = pl.ds(pl.multiple_of(start * CAP, CAP), size * CAP)
                value = jnp.dot(hid[at, :], wd[h], preferred_element_type=jnp.float32)
                back_units[h, pl.ds(start, size)] = value.reshape(size, CAP, half).astype(
                    jnp.bfloat16
                )

            chunked(n_units, SPAN, lower)
            for dm in range(1, SPAN):
                returns[dm, h] = begin(
                    back.at[h, dm], shares.at[h, dm], q_send.at[n, h * SPAN + dm],
                    q_recv.at[n, h * SPAN + dm], member(SPAN - dm, 0),
                )
        return returns

    def reduce(dd, bufs, returns):
        settle([returns[dm, dd] for dm in range(SPAN) if (dm, dd) in returns])
        total = None
        for dm in range(SPAN):
            src = bufs[3] if dm == 0 else bufs[4]
            value = src[dd, dm].astype(jnp.float32)
            total = value if total is None else total + value
        return total.astype(jnp.bfloat16)

    swaps = []
    near_copies = spread(0, 0, near_bufs[0]) + spread(0, 1, near_bufs[0])
    for i, (src, dst) in enumerate(((wg_hbm, wg), (wu_hbm, wu), (wd_hbm, wd))):
        for dd in range(1, n_dp):
            swaps.append(
                begin(src.at[0], dst.at[core], w_send.at[i], w_recv.at[i], member(0, dd))
            )
    far_copies = []
    for dd in range(n_dp):
        settle([to_groups[dd, r] for r in range(1, n_groups)])
        far_copies += spread(1, dd, far_bufs[0])
    for load in loads[1:]:
        load.wait()
    settle(swaps + near_copies)
    near_returns = work_on(0, 0, 1, near_bufs)
    settle(far_copies)
    far_returns = work_on(1, 1, n_far, far_bufs)
    for dd in range(n_dp):
        final[dd, pl.ds(0, 1)] = reduce(dd, near_bufs, near_returns)
    homeward = []
    for dd in range(n_dp):
        summed[dd] = reduce(dd, far_bufs, far_returns)
        for r in range(1, n_groups):
            homeward.append(
                begin(
                    summed.at[dd, r - 1], final.at[dd, r], c_send.at[dd, r - 1],
                    c_recv.at[dd, r - 1], group_peer(n_groups - r),
                )
            )
    for dd in range(n_dp):
        settle(homeward[dd * n_far : (dd + 1) * n_far])
        at = dd * half
        block = final[dd].astype(jnp.float32).reshape(n_groups * CAP, half)
        out_ref[:, at : at + half] = block.astype(jnp.bfloat16)
    for copy in started:
        copy.wait_send()


def body(tokens, group_ids, expert_ids, gate_weights, gate_proj, up_proj, down_proj):
    tok_rows, width = tokens.shape
    n_groups = lax.axis_size("expert") // SPAN
    n_dp = lax.axis_size("dp")
    half = gate_proj.shape[1]
    cols = gate_proj.shape[2]
    lanes = -(-n_groups * GROUP_EXP // LANES) * LANES
    low, full = jnp.bfloat16, jnp.float32
    vmem = pl.BlockSpec(memory_space=pltpu.VMEM)
    hbm = pl.BlockSpec(memory_space=pl.ANY)
    dma = pltpu.SemaphoreType.DMA
    spots = n_dp * SPAN

    def buffers(count):
        n_rows = SPAN * count * CAP
        return (
            pltpu.VMEM((SPAN, count, CAP, width + lanes), low),
            pltpu.VMEM((2, n_rows, cols), full),
            pltpu.VMEM((n_rows, cols), low),
            pltpu.VMEM((n_dp, SPAN, count, CAP, half), low),
            pltpu.VMEM((n_dp, SPAN, count, CAP, half), low),
        )

    parts, select = pl.pallas_call(
        functools.partial(kernel, n_groups, n_dp),
        out_shape=(
            jax.ShapeDtypeStruct((n_groups * CAP, width), low),
            jax.ShapeDtypeStruct((n_groups * CAP, tok_rows), low),
        ),
        in_specs=[vmem, vmem, vmem, hbm, hbm, hbm, hbm],
        out_specs=(vmem, vmem),
        scratch_shapes=[
            pltpu.VMEM((tok_rows, width), low),
            pltpu.VMEM((n_dp, cols, half), low),
            pltpu.VMEM((n_dp, cols, half), low),
            pltpu.VMEM((n_dp, cols, half), low),
            pltpu.VMEM((n_groups, CAP, width + lanes), low),
            pltpu.VMEM((n_groups - 1, CAP, width + lanes), low),
            pltpu.VMEM((n_dp, n_groups - 1, CAP, half), low),
            pltpu.VMEM((n_dp, n_groups, CAP, half), low),
            buffers(1),
            buffers(n_groups - 1),
            dma((4,)), dma((2, 2)),
            dma((n_dp, n_groups - 1)), dma((n_dp, n_groups - 1)),
            dma((2, spots)), dma((2, spots)),
            dma((3,)), dma((3,)),
            dma((2, spots)), dma((2, spots)),
            dma((n_dp, n_groups - 1)), dma((n_dp, n_groups - 1)),
        ],
        compiler_params=pltpu.CompilerParams(
            collective_id=0, has_side_effects=True, vmem_limit_bytes=60 * 1024 * 1024
        ),
    )(group_ids.T, expert_ids.T, gate_weights.T, tokens,
      *(jnp.swapaxes(w, 1, 2) for w in (gate_proj, up_proj, down_proj)))
    result = lax.dot_general(
        select, parts, (((0,), (0,)), ((), ())), preferred_element_type=jnp.float32
    )
    return result.astype(low)


def solution(mesh):
    placed = (
        P(("groups", "expert", "dp"), None),
        P(("groups", "expert", "dp"), None),
        P(("groups", "expert", "dp"), None),
        P(("groups", "expert", "dp"), None),
        P("expert", "dp", None),
        P("expert", "dp", None),
        P("expert", "dp", None),
    )
    return jax.shard_map(
        body,
        mesh=mesh,
        in_specs=placed,
        out_specs=P(("groups", "expert", "dp"), None),
        check_vma=False,
    )
```

time: 28.5 us -> 28.7 us (level)
  no operation moved by 1% of the time
where the time goes in v5:
time: 28.7 us; the launch traced here: 28.5 us
  Pallas kernels  26.6 us (93%)
  matrix products  1.88 us (7%)
    pallas_call x1, Pallas kernels, body(): pl.pallas_call(functools.partial(kernel, n_groups, n_dp), out_shape=(jax....  26.6 us
    dot_general x1, matrix products, body(): lax.dot_general(select, parts, (((0,), (0,)), ((), ())), preferred_elemen...  1.88 us

profile of v5, /device:TPU:0, one launch (start us, length us, event | category | flops | bytes accessed | tf_op | source)
XLA Modules:
  0.0 28.5 jit_solution(14349419519523913485)
XLA Ops:
  0.0 26.6 %shard_map.73 = (bf16[16,2560]{1,0:T(8,128)(2,1)}, bf16[16,64]{1,0:T(8,128)(2,1)}) custom-call(s32[2,64]{1,0:T(2,128)} %bitcast.13, s32[6,64]{1,0:T(8,128)} %bitcast.11, bf16[6,64]{1,0:T(8,128)(2,1)} %bitcast.12, bf16[64,2560]{1,0:T(8,128)(2,1)} %tok_hbm.1, bf16[1,576,1280]{2,1,0:T(8,128)(2,1)} %bitcast.8, bf16[1,576,1280]{2,1,0:T(8,128)(2,1)} %bitcast.9, ...), custom_call_target="tpu_custom_call" | custom-call | tf_op jit(solution)/shard_map/pallas_call | solution.py:284
  26.6 1.9 %convolution_convert_fusion = bf16[64,2560]{1,0:T(8,128)(2,1)} fusion(bf16[16,64]{1,0:T(8,128)(2,1)} %get-tuple-element.7, bf16[16,2560]{1,0:T(8,128)(2,1)} %get-tuple-element.8), kind=kOutput, calls=%fused_computation | convolution fusion | flops 5406720 | bytes 411648 | tf_op jit(solution)/shard_map/dot_general | solution.py:315
